TPU v7x, 128 devices: a whole 4x4x4 slice. The times are simulated.
128 devices in a mesh: dp: 8 (over y_lo, z), expert: 16 (over y_hi, x, core).
Axes of the slice: x: 4, y: 4 (y_hi: 2, y_lo: 2; y = y_hi * 2 + y_lo), z: 4, core: 2. Of those that a mesh axis runs over, the one named last changes fastest.
Arguments:
- tokens: bfloat16 [256, 768, 1024], P(None, ('dp', 'expert')), may hold values from -200 to 200
- grad_out: bfloat16 [256, 768, 1024], P(None, ('dp', 'expert')), may hold values from -6 to 6
- slot_out: bfloat16 [512, 768, 1024], P('expert', 'dp'), may hold values from -6 to 6
- slot_params: bfloat16 [512, 1024], P('expert'), may hold values from -2 to 2
Outputs:
- grad_tokens: bfloat16 [256, 768, 1024], P(None, ('dp', 'expert'))
- grad_slot_out: bfloat16 [512, 768, 1024], P('expert', 'dp')
- grad_params: float32 [512, 1024], P('expert', 'dp')
All inputs are finite; a program needn't handle non-finite values.
Results may differ from a plain program's by a relative error of at most 0.018.
Values may be sent and summed in bfloat16 or wider, within the bound.
A program may use at most 128 MiB of HBM per device.

v0:
```python
import jax
import jax.numpy as jnp
from jax import lax
from jax.sharding import PartitionSpec as P


def sent_to_all(value, axis):
    length = lax.axis_size(axis)
    return lax.all_to_all(
        jnp.broadcast_to(value[None], (length, *value.shape)), axis, 0, 0, tiled=True
    )


def in_order(pieces, dim):
    pieces = jnp.moveaxis(pieces, 0, dim)
    lengths = pieces.shape
    return pieces.reshape(*lengths[:dim], lengths[dim] * lengths[dim + 1], *lengths[dim + 2 :])


def gathered_copies(value, axis, dim):
    pieces = sent_to_all(value, axis)
    return in_order(pieces, dim)


def split_up(value, dim, length):
    lengths = value.shape
    pieces = value.reshape(*lengths[:dim], length, lengths[dim] // length, *lengths[dim + 1 :])
    return jnp.moveaxis(pieces, dim, 0)


def sum_at_owner(value, axis, dim):
    pieces = split_up(value, dim, lax.axis_size(axis))
    arrived = lax.all_to_all(pieces, axis, split_axis=0, concat_axis=0, tiled=True)
    return arrived.astype(jnp.float32).sum(axis=0)


def fetch_outputs(slot_out, owners):
    own_slots, img_all, width = slot_out.shape
    shaped = slot_out.reshape(own_slots, owners, img_all // owners, width)
    arrived = lax.all_to_all(shaped, "expert", split_axis=1, concat_axis=0, tiled=True)
    return arrived.reshape(own_slots * owners, img_all // owners, width)


def return_grads(grad_slot, owners):
    all_slots, img_rows, width = grad_slot.shape
    shaped = grad_slot.reshape(owners, all_slots // owners, img_rows, width)
    arrived = lax.all_to_all(shaped, "expert", split_axis=0, concat_axis=2, tiled=True)
    return arrived.reshape(all_slots // owners, owners * img_rows, width)


def logit_grads(grad_comb, combine):
    rowdot = jnp.sum(combine * grad_comb, axis=-1, keepdims=True)
    return (combine * (grad_comb - rowdot)).astype(jnp.bfloat16)


def per_device(tokens, grad_out, slot_out, slot_params):
    owners = lax.axis_size("expert")
    all_params = gathered_copies(slot_params, "expert", 0)
    logits = jnp.einsum("tbd,sd->tbs", tokens, all_params, preferred_element_type=jnp.float32)
    combine = jax.nn.softmax(logits, axis=-1)
    combine_low = combine.astype(jnp.bfloat16)
    slot_rows = fetch_outputs(slot_out, owners)
    grad_slot = jnp.einsum(
        "tbs,tbd->sbd", combine_low, grad_out, preferred_element_type=jnp.float32
    ).astype(jnp.bfloat16)
    grad_slot_out = return_grads(grad_slot, owners)
    grad_comb = jnp.einsum("tbd,sbd->tbs", grad_out, slot_rows, preferred_element_type=jnp.float32)
    grad_logits = logit_grads(grad_comb, combine)
    grad_tok = jnp.einsum(
        "tbs,sd->tbd", grad_logits, all_params, preferred_element_type=jnp.float32
    ).astype(jnp.bfloat16)
    param_part = jnp.einsum("tbs,tbd->sd", grad_logits, tokens, preferred_element_type=jnp.float32)
    owned = lax.psum_scatter(
        param_part.astype(jnp.bfloat16), "expert", scatter_dimension=0, tiled=True
    )
    grad_params = sum_at_owner(owned, "dp", 1)
    return (grad_tok, grad_slot_out, grad_params)


def solution(mesh):
    return jax.shard_map(
        per_device,
        mesh=mesh,
        in_specs=(
            P(None, ("dp", "expert"), None),
            P(None, ("dp", "expert"), None),
            P("expert", "dp", None),
            P("expert", None),
        ),
        out_specs=(P(None, ("dp", "expert"), None), P("expert", "dp", None), P("expert", "dp")),
        check_vma=False,
    )
```

profile of v0, /device:TPU:1, one launch (start us, length us, event | category | flops | bytes accessed | tf_op | source)
XLA Modules:
  0.0 261.5 jit_solution(3334196469402528073)
XLA Ops:
  7.2 0.0 copy-start
  7.2 2.1 broadcast_in_dim.2
  9.3 8.4 %all-to-all-start = ((bf16[16,32,1024]{2,1,0:T(8,128)(2,1)}), bf16[16,32,1024]{2,1,0:T(8,128)(2,1)}, u32[]{:S(2)}, u32[]{:S(2)}) async-start(bf16[16,32,1024]{2,1,0:T(8,128)(2,1)} %broadcast_in_dim.2), calls=%async_computation | async-start | bytes 2097152 | tf_op jit(solution)/shard_map/all_to_all | solution.py:9
  17.7 9.0 %copy.19 = bf16[32,96,1024]{2,0,1:T(8,128)(2,1)} copy(bf16[32,96,1024]{2,1,0:T(8,128)(2,1)} %param.6) | data formatting | bytes 12582912 | tf_op args[2]
  26.7 8.4 %all-to-all-done = bf16[16,32,1024]{2,1,0:T(8,128)(2,1)} async-done(((bf16[16,32,1024]{2,1,0:T(8,128)(2,1)}), bf16[16,32,1024]{2,1,0:T(8,128)(2,1)}, u32[]{:S(2)}, u32[]{:S(2)}) %all-to-all-start) | async-done | bytes 1048608 | tf_op jit(solution)/shard_map/all_to_all | solution.py:9
  35.1 5.1 %all-to-all-start.1 = ((bf16[32,16,6,1024]{3,0,2,1:T(8,128)(2,1)}), bf16[32,16,6,1024]{3,0,2,1:T(8,128)(2,1)}, u32[]{:S(2)}, u32[]{:S(2)}) async-start(bf16[32,16,6,1024]{3,0,2,1:T(8,128)(2,1)} %bitcast.45), calls=%async_computation.1 | async-start | bytes 12582912 | tf_op jit(solution)/shard_map/all_to_all | solution.py:40
  40.2 4.1 %fusion.6 = f32[256,6,512]{2,0,1:T(8,128)S(1)} fusion(bf16[256,6,1024]{2,0,1:T(8,128)(2,1)} %param.4, bf16[512,1024,1]{1,0,2:T(8,128)(2,1)} %bitcast.1), kind=kOutput, calls=%fused_computation.15 | convolution fusion | flops 1610612736 | bytes 7340032 | tf_op jit(solution)/shard_map/tbd,sd->tbs/dot_general | solution.py:59
  44.3 0.0 copy-start.2
  44.3 2.6 fusion.5
  46.9 0.1 copy-done.2
  47.0 0.0 copy-done
  47.0 11.5 %convolution_convert_fusion = bf16[6,512,1024]{2,1,0:T(8,128)(2,1)} fusion(bf16[256,6,1024]{2,0,1:T(8,128)(2,1)S(1)} %copy-done, f32[256,6]{0,1:T(8,128)S(1)} %get-tuple-element.9, f32[256,6,512]{2,0,1:T(8,128)} %copy-done.2), kind=kOutput, calls=%fused_computation.1 | convolution fusion | flops 1616119808 | bytes 12589056 | tf_op jit(solution)/shard_map/tbs,tbd->sbd/dot_general | solution.py:63
  58.5 6.7 %copy.23 = bf16[16,32,6,1024]{3,1,2,0:T(8,128)(2,1)} copy(bf16[16,32,6,1024]{3,1,0,2:T(8,128)(2,1)} %bitcast.47) | data formatting | bytes 12582912 | tf_op jit(solution)/shard_map/reshape | solution.py:46
  65.2 59.0 %all-to-all-done.1 = bf16[32,16,6,1024]{3,0,2,1:T(8,128)(2,1)} async-done(((bf16[32,16,6,1024]{3,0,2,1:T(8,128)(2,1)}), bf16[32,16,6,1024]{3,0,2,1:T(8,128)(2,1)}, u32[]{:S(2)}, u32[]{:S(2)}) %all-to-all-start.1) | async-done | bytes 6291488 | tf_op jit(solution)/shard_map/all_to_all | solution.py:40
  124.2 6.5 %all-to-all-start.2 = ((bf16[16,32,6,1024]{3,1,2,0:T(8,128)(2,1)}), bf16[16,32,6,1024]{3,1,2,0:T(8,128)(2,1)}, u32[]{:S(2)}, u32[]{:S(2)}) async-start(bf16[16,32,6,1024]{3,1,2,0:T(8,128)(2,1)} %copy.23), calls=%async_computation.2 | async-start | bytes 12582912 | tf_op jit(solution)/shard_map/all_to_all | solution.py:47
  130.8 0.2 reduce-scatter.2.cloned.1.call-start
  131.0 0.0 copy-start.1
  131.0 3.7 %copy.20 = bf16[16,32,1,6,1024]{4,1,0,3,2:T(8,128)(2,1)S(1)} copy(bf16[16,32,1,6,1024]{4,1,3,0,2:T(8,128)(2,1)} %bitcast.4) | data formatting | bytes 12582912 | tf_op jit(solution)/shard_map/all_to_all | solution.py:40
  134.6 0.0 copy-done.1
  134.7 2.0 fusion.1
  136.7 0.0 copy-start.4
  136.7 0.6 fusion.3
  137.3 0.0 copy-start.3
  137.3 1.1 copy-done.3
  138.5 0.7 copy-done.4
  139.1 2.8 %bitcast_convert_fusion = bf16[512,1024]{1,0:T(8,128)(2,1)} fusion(bf16[256,6,512]{2,0,1:T(8,128)(2,1)S(1)} %fusion.3, bf16[256,6,1024]{2,0,1:T(8,128)(2,1)S(1)} %copy-done.4), kind=kOutput, calls=%fused_computation.9 | convolution fusion | flops 1611137024 | bytes 5767168 | tf_op jit(solution)/shard_map/tbs,tbd->sd/dot_general | solution.py:72
  141.9 0.0 reduce-scatter.2.cloned.1.call-update
  141.9 91.8 %reduce-scatter.2.cloned.1.call-done = bf16[32,1024]{1,0:T(8,128)(2,1)} async-done(((bf16[512,1024]{1,0:T(8,128)(2,1)}), bf16[32,1024]{1,0:T(8,128)(2,1)}) %reduce-scatter.2.cloned.1.call-update) | async-done | bytes 65552 | tf_op jit(solution)/shard_map/reduce_scatter | solution.py:73
  233.8 1.5 bitcast_bitcast_fusion
  235.2 0.0 all-to-all-done.2
  235.2 4.6 %all-to-all-start.3 = ((bf16[8,32,128]{2,1,0:T(8,128)(2,1)}), bf16[8,32,128]{2,1,0:T(8,128)(2,1)S(1)}, u32[]{:S(2)}, u32[]{:S(2)}) async-start(bf16[8,32,128]{2,1,0:T(8,128)(2,1)} %bitcast_bitcast_fusion), calls=%async_computation.4 | async-start | bytes 131072 | tf_op jit(solution)/shard_map/all_to_all | solution.py:33
  239.9 5.2 %convolution_convert_fusion.1 = bf16[256,6,1024]{2,0,1:T(8,128)(2,1)} fusion(bf16[256,6,512]{2,0,1:T(8,128)(2,1)} %copy-done.3, bf16[512,1024,1]{1,0,2:T(8,128)(2,1)} %bitcast.1), kind=kOutput, calls=%fused_computation.8 | convolution fusion | flops 1612185600 | bytes 5767168 | tf_op jit(solution)/shard_map/tbs,sd->tbd/dot_general | solution.py:69
  245.0 9.0 %copy.26 = bf16[32,96,1024]{2,1,0:T(8,128)(2,1)} copy(bf16[32,96,1024]{2,0,1:T(8,128)(2,1)} %bitcast.11) | data formatting | bytes 12582912
  254.0 0.0 all-to-all-done.3
  254.0 0.6 convert_reduce_fusion
Async XLA Ops:
  7.2 39.8 %copy-start = (bf16[256,6,1024]{2,0,1:T(8,128)(2,1)S(1)}, bf16[256,6,1024]{2,0,1:T(8,128)(2,1)}, u32[]{:S(2)}) copy-start(bf16[256,6,1024]{2,0,1:T(8,128)(2,1)} %param.5) | copy-start | bytes 9437188
  9.3 25.8 %all-to-all-start = ((bf16[16,32,1024]{2,1,0:T(8,128)(2,1)}), bf16[16,32,1024]{2,1,0:T(8,128)(2,1)}, u32[]{:S(2)}, u32[]{:S(2)}) async-start(bf16[16,32,1024]{2,1,0:T(8,128)(2,1)} %broadcast_in_dim.2), calls=%async_computation | async-start | bytes 2097152 | tf_op jit(solution)/shard_map/all_to_all | solution.py:9
  35.1 89.1 %all-to-all-start.1 = ((bf16[32,16,6,1024]{3,0,2,1:T(8,128)(2,1)}), bf16[32,16,6,1024]{3,0,2,1:T(8,128)(2,1)}, u32[]{:S(2)}, u32[]{:S(2)}) async-start(bf16[32,16,6,1024]{3,0,2,1:T(8,128)(2,1)} %bitcast.45), calls=%async_computation.1 | async-start | bytes 12582912 | tf_op jit(solution)/shard_map/all_to_all | solution.py:40
  44.3 2.7 %copy-start.2 = (f32[256,6,512]{2,0,1:T(8,128)}, f32[256,6,512]{2,0,1:T(8,128)S(1)}, u32[]{:S(2)}) copy-start(f32[256,6,512]{2,0,1:T(8,128)S(1)} %fusion.6) | copy-start | bytes 9437188
  124.2 111.0 %all-to-all-start.2 = ((bf16[16,32,6,1024]{3,1,2,0:T(8,128)(2,1)}), bf16[16,32,6,1024]{3,1,2,0:T(8,128)(2,1)}, u32[]{:S(2)}, u32[]{:S(2)}) async-start(bf16[16,32,6,1024]{3,1,2,0:T(8,128)(2,1)} %copy.23), calls=%async_computation.2 | async-start | bytes 12582912 | tf_op jit(solution)/shard_map/all_to_all | solution.py:47
  130.8 103.0 %reduce-scatter.2.cloned.1.call-start = ((), (), s32[]{:S(2)}) async-start(), calls=%async_computation.5 | async-start | bytes 1114112 | tf_op jit(solution)/shard_map/reduce_scatter | solution.py:73
  131.0 3.7 %copy-start.1 = (f32[256,6,512]{2,0,1:T(8,128)S(1)}, f32[256,6,512]{2,0,1:T(8,128)}, u32[]{:S(2)}) copy-start(f32[256,6,512]{2,0,1:T(8,128)} %get-tuple-element.10) | copy-start | bytes 9437188
  136.7 2.5 copy-start.4
  137.3 1.1 copy-start.3
  235.2 18.8 %all-to-all-start.3 = ((bf16[8,32,128]{2,1,0:T(8,128)(2,1)}), bf16[8,32,128]{2,1,0:T(8,128)(2,1)S(1)}, u32[]{:S(2)}, u32[]{:S(2)}) async-start(bf16[8,32,128]{2,1,0:T(8,128)(2,1)} %bitcast_bitcast_fusion), calls=%async_computation.4 | async-start | bytes 131072 | tf_op jit(solution)/shard_map/all_to_all | solution.py:33
Sparse Core Ops, SparseCore 0:
  142.1 91.6 reduce-scatter.1
where the time goes:
time: 264 us; the launch traced here: 261 us
  waiting for transfers between devices  159 us (60%)
  local copies, waits for them, and re-layouts  33.9 us (13%)
  matrix products  25.5 us (10%)
  starting transfers between devices  25 us (9%)
  between operations  14.1 us (5%)
  other arithmetic  3.8 us (1%)
    reduce_scatter x1, waiting for transfers between devices, per_device(): lax.psum_scatter(param_part.astype(jnp.bfloat16), 'expert', scatter_dimen...  91.8 us
    all_to_all x1, waiting for transfers between devices, fetch_outputs(): lax.all_to_all(shaped, 'expert', split_axis=1, concat_axis=0, tiled=True)  59 us
    unnamed x12, local copies, waits for them, and re-layouts  19.9 us
    dot_general x1, matrix products, per_device(): jnp.einsum('tbs,tbd->sbd', combine_low, grad_out, preferred_element_type=...  11.5 us
    all_to_all x1, starting transfers between devices, sent_to_all(): lax.all_to_all(jnp.broadcast_to(value[None], (length, *value.shape)), axi...  8.44 us
    all_to_all x1, waiting for transfers between devices, sent_to_all(): lax.all_to_all(jnp.broadcast_to(value[None], (length, *value.shape)), axi...  8.37 us
    reshape x1, local copies, waits for them, and re-layouts, return_grads(): shaped = grad_slot.reshape(owners, all_slots // owners, img_rows, width)  6.72 us
    all_to_all x1, starting transfers between devices, return_grads(): lax.all_to_all(shaped, 'expert', split_axis=0, concat_axis=2, tiled=True)  6.55 us
  transfers between devices with their start and end apart: 5, of which 3 were waited for; matrix products, arithmetic and copies ran while one was open for 22% of the time, Pallas kernels for 0%

commit v1 on v0

v1 whole, which is shorter than its diff:
```python
import functools

import jax
import jax.numpy as jnp
from jax import lax
from jax.experimental import pallas as pl
from jax.experimental.pallas import tpu as pltpu
from jax.sharding import PartitionSpec as P

MESH = pl.DeviceIdType.MESH
BF = jnp.bfloat16
F32 = jnp.float32

ROWS, XS, CORES = 2, 4, 2
NEAR, ZS = 2, 4
CHIPS = ROWS * XS
STEPS = ((1, 0), (1, 2), (0, 1), (0, 3), (1, 1), (1, 3), (0, 2))
ORDER = tuple((r, x, c) for c in range(CORES) for r, x in STEPS) + ((0, 0, 1),)
NT = (((1,), (1,)), ((), ()))
TN = (((0,), (0,)), ((), ()))


def dot(a, b, dims):
    return lax.dot_general(a, b, dims, preferred_element_type=F32)


def row_order(own, lanes, flip):
    n = own * lanes
    r = lax.broadcasted_iota(jnp.int32, (n, n), 0)
    c = lax.broadcasted_iota(jnp.int32, (n, n), 1)
    if flip:
        hit = c == (r % lanes) * own + r // lanes
    else:
        hit = c == (r % own) * lanes + r // own
    return jnp.where(hit, 1.0, 0.0).astype(BF)


def exchange(
    tok_hbm, go_hbm, so_hbm, sp_hbm,
    gso, gt, gp,
    tok, go, raw, send_a, recv_a, send_b, par, comb, pp, perm,
    r1s, r1r, acc, r2s, r2r, r3s, r3r, r4s, r4r,
    so_sem, in_sem, par_s, par_r, as_sem, ar_sem, bs_sem, br_sem, own_sem, red_s, red_r,
):
    imgs, width = tok.shape[0], tok.shape[2]
    blocks, own, lanes = raw.shape[0], so_hbm.shape[0], so_hbm.shape[2]
    slots = CHIPS * CORES * own
    tokens = tok.shape[1]
    d = lax.axis_index("dp")
    e = lax.axis_index("expert")
    row, x, c = e // (XS * CORES), (e // CORES) % XS, e % CORES
    chip = e // CORES
    near, z = d // ZS, d % ZS

    def peer(dr, dx, dc):
        return ((row + dr) % ROWS) * (XS * CORES) + ((x + dx) % XS) * CORES + (c + dc) % CORES

    def zpeer(k):
        return (near * ZS + (z + k) % ZS, e)

    side = ((1 - near) * ZS + z, e)
    partner = (d, peer(0, 0, 1))

    barrier = pltpu.get_barrier_semaphore()
    others = [(d, peer(*o)) for o in ORDER] + [zpeer(k) for k in range(1, ZS)] + [side]
    for dev in others:
        pl.semaphore_signal(barrier, inc=1, device_id=dev, device_id_type=MESH)

    def load_so(g):
        return pltpu.make_async_copy(so_hbm.at[:, g], raw.at[g], so_sem.at[g])

    sp_in = pltpu.make_async_copy(sp_hbm.at[z], par.at[chip, c, z], in_sem.at[0])
    tok_in = pltpu.make_async_copy(tok_hbm, tok, in_sem.at[1])
    go_in = pltpu.make_async_copy(go_hbm, go, in_sem.at[2])
    sp_in.start()
    for g in range(blocks):
        load_so(g).start()
    tok_in.start()
    go_in.start()
    perm[...] = row_order(own, lanes, False)

    pl.semaphore_wait(barrier, len(others))

    def remote(src, dst, s, r, dev):
        return pltpu.make_async_remote_copy(
            src_ref=src, dst_ref=dst, send_sem=s, recv_sem=r, device_id=dev, device_id_type=MESH
        )

    def par_row(i):
        r, dx = STEPS[i]
        piece = par.at[chip, c, z]
        return remote(piece, piece, par_s.at[i], par_r.at[i], (d, peer(r, dx, 0)))

    def par_z(k):
        piece = par.at[:, c, z]
        n = len(STEPS) + k - 1
        return remote(piece, piece, par_s.at[n], par_r.at[n], zpeer(k))

    def par_core():
        piece = par.at[:, c]
        n = len(STEPS) + ZS - 1
        return remote(piece, piece, par_s.at[n], par_r.at[n], partner)

    sp_in.wait()
    for i in range(len(STEPS)):
        par_row(i).start()

    @pl.loop(0, blocks)
    def _(g):
        load_so(g).wait()
        block = raw.at[g].reshape(own * lanes, width)
        out = send_a.at[pl.ds(g * lanes, lanes)].reshape(own * lanes, width)
        for n in range(0, width, 256):
            out[:, n : n + 256] = dot(perm[...], block[:, n : n + 256], (((1,), (0,)), ((), ()))).astype(BF)

    def send_out(j, o):
        p = peer(*o)
        return remote(
            send_a.at[p * imgs + j], recv_a.at[j, e], as_sem.at[j], ar_sem.at[j], (d, p)
        )

    def keep_out(j):
        return pltpu.make_async_copy(send_a.at[e * imgs + j], recv_a.at[j, e], own_sem.at[0, j])

    def send_back(j, o):
        p = peer(*o)
        return remote(
            send_b.at[j, p], gso.at[e * imgs + j], bs_sem.at[j], br_sem.at[j], (d, p)
        )

    def keep_back(j):
        return pltpu.make_async_copy(send_b.at[j, e], gso.at[e * imgs + j], own_sem.at[1, j])

    @pl.loop(0, imgs)
    def _(j):
        for o in ORDER:
            send_out(j, o).start()
        keep_out(j).start()

    for i in range(len(STEPS)):
        par_row(i).wait_recv()
    for k in range(1, ZS):
        par_z(k).start()
    for k in range(1, ZS):
        par_z(k).wait_recv()
    par_core().start()
    par_core().wait_recv()
    tok_in.wait()
    go_in.wait()

    params = par.reshape(slots, width)

    @pl.loop(0, imgs)
    def _(j):
        logits = dot(params[...], tok[j], NT)
        top = jnp.max(logits, axis=0, keepdims=True)
        raised = jnp.exp(logits - top)
        weight = raised / jnp.sum(raised, axis=0, keepdims=True)
        comb[j] = weight
        low = weight.astype(BF)
        out = send_b.at[j].reshape(slots, width)
        for n in range(0, width, 256):
            out[:, n : n + 256] = dot(low, go[j, :, n : n + 256], (((1,), (0,)), ((), ()))).astype(BF)

        @pl.when(j > 0)
        def _():
            for o in ORDER:
                send_back(j - 1, o).start()
            keep_back(j - 1).start()

    pp[...] = jnp.zeros_like(pp)
    for o in ORDER:
        send_back(imgs - 1, o).start()
    keep_back(imgs - 1).start()

    def all_of(ref, sem):
        return pltpu.make_async_copy(ref, ref, sem)

    @pl.loop(0, imgs)
    def _(j):
        all_of(recv_a.at[j, pl.ds(0, len(ORDER))], ar_sem.at[j]).wait()
        keep_out(j).wait()
        rows = recv_a.at[j].reshape(slots, width)
        grad = dot(rows[...], go[j], NT)
        weight = comb[j]
        rowdot = jnp.sum(weight * grad, axis=0, keepdims=True)
        low = (weight * (grad - rowdot)).astype(BF)
        for n in range(0, width, 256):
            pp[:, n : n + 256] += dot(low, tok[j, :, n : n + 256], (((1,), (0,)), ((), ())))
            gt[j, :, n : n + 256] = dot(low, params[:, n : n + 256], TN).astype(BF)

    share = pp.reshape(CHIPS, CORES, own, width)
    r1s[...] = share[:, 1 - c].astype(BF)
    over_core = remote(r1s, r1r, red_s.at[0], red_r.at[0], partner)
    over_core.start()
    over_core.wait_recv()
    half = (share[:, c] + r1r[...].astype(F32)).reshape(CHIPS * own, width)
    piece = width // (NEAR * ZS)
    for n in range(NEAR):
        for k in range(ZS):
            m = (n * ZS + k) * piece
            acc[k, n] = half[:, m : m + piece]
    r2s[...] = acc[...].astype(BF)

    def over_z(k):
        return remote(r2s.at[(z + k) % ZS], r2r.at[k - 1], red_s.at[k], red_r.at[k], zpeer(k))

    for k in range(1, ZS):
        over_z(k).start()
    total = acc[z]
    for k in range(1, ZS):
        over_z(k).wait_recv()
        total = total + r2r[k - 1].astype(F32)
    acc[0] = total
    r3s[...] = acc[0, 1 - near].astype(BF)
    over_side = remote(r3s, r3r, red_s.at[ZS], red_r.at[ZS], side)
    over_side.start()
    over_side.wait_recv()
    mine = (acc[0, near] + r3r[...].astype(F32)).reshape(CHIPS, own, piece)
    r4s[...] = mine.astype(BF)
    acc[1, 0] = mine.reshape(CHIPS * own, piece)

    def over_chips(i):
        p = peer(*STEPS[i], 0)
        return remote(r4s.at[p // CORES], r4r.at[i], red_s.at[ZS + 1 + i], red_r.at[ZS + 1 + i], (d, p))

    for i in range(len(STEPS)):
        over_chips(i).start()
    owned = acc.at[1, 0].reshape(CHIPS, own, piece)[chip]
    for i in range(len(STEPS)):
        over_chips(i).wait_recv()
        owned = owned + r4r[i].astype(F32)
    gp[...] = owned

    for i in range(len(STEPS)):
        par_row(i).wait_send()
        over_chips(i).wait_send()
    for k in range(1, ZS):
        par_z(k).wait_send()
        over_z(k).wait_send()
    par_core().wait_send()
    over_core.wait_send()
    over_side.wait_send()

    @pl.loop(0, imgs)
    def _(j):
        all_of(send_a.at[pl.ds(0, len(ORDER))], as_sem.at[j]).wait()
        all_of(send_b.at[j, pl.ds(0, len(ORDER))], bs_sem.at[j]).wait()
        keep_back(j).wait()
        all_of(gso.at[pl.ds(0, len(ORDER))], br_sem.at[j]).wait()


def settle(gso, gt, gp, gso_out, gt_out, gp_out, perm, stage, sems):
    lanes, own = gso_out.shape[2], gso_out.shape[0]
    width = gso_out.shape[3]
    blocks = gso_out.shape[1]
    gt_copy = pltpu.make_async_copy(gt, gt_out, sems.at[0])
    gp_copy = pltpu.make_async_copy(gp, gp_out, sems.at[1])
    gt_copy.start()
    gp_copy.start()
    perm[...] = row_order(own, lanes, True)

    def put(g):
        return pltpu.make_async_copy(stage.at[g], gso_out.at[:, g], sems.at[2 + g])

    @pl.loop(0, blocks)
    def _(g):
        block = gso.at[pl.ds(g * lanes, lanes)].reshape(own * lanes, width)
        out = stage.at[g].reshape(own * lanes, width)
        for n in range(0, width, 256):
            out[:, n : n + 256] = dot(perm[...], block[:, n : n + 256], (((1,), (0,)), ((), ()))).astype(BF)
        put(g).start()

    @pl.loop(0, blocks)
    def _(g):
        put(g).wait()

    gt_copy.wait()
    gp_copy.wait()


def per_device(tokens, grad_out, slot_out, slot_params):
    toks, imgs, width = tokens.shape
    own, all_imgs, _ = slot_out.shape
    lanes = 8
    blocks = all_imgs // lanes
    slots = CHIPS * CORES * own
    tok = jnp.swapaxes(tokens, 0, 1)
    go = jnp.swapaxes(grad_out, 0, 1)
    so = slot_out.reshape(own, blocks, lanes, width)
    sp = slot_params.reshape(ZS, own // ZS, width)
    piece = width // (NEAR * ZS)
    anywhere = pl.BlockSpec(memory_space=pl.ANY)
    vmem = pl.BlockSpec(memory_space=pltpu.VMEM)
    dma = pltpu.SemaphoreType.DMA
    peers = len(ORDER)
    gso, gt, gp = pl.pallas_call(
        exchange,
        out_shape=(
            pltpu.VMEM((all_imgs, own, width), BF),
            pltpu.VMEM((imgs, toks, width), BF),
            pltpu.VMEM((own, piece), F32),
        ),
        in_specs=[anywhere] * 4,
        out_specs=(vmem, vmem, vmem),
        scratch_shapes=[
            pltpu.VMEM((imgs, toks, width), BF),
            pltpu.VMEM((imgs, toks, width), BF),
            pltpu.VMEM((blocks, own, lanes, width), BF),
            pltpu.VMEM((all_imgs, own, width), BF),
            pltpu.VMEM((imgs, CHIPS * CORES, own, width), BF),
            pltpu.VMEM((imgs, CHIPS * CORES, own, width), BF),
            pltpu.VMEM((CHIPS, CORES, ZS, own // ZS, width), BF),
            pltpu.VMEM((imgs, slots, toks), F32),
            pltpu.VMEM((slots, width), F32),
            pltpu.VMEM((own * lanes, own * lanes), BF),
            pltpu.VMEM((CHIPS, own, width), BF),
            pltpu.VMEM((CHIPS, own, width), BF),
            pltpu.VMEM((ZS, NEAR, CHIPS * own, piece), F32),
            pltpu.VMEM((ZS, NEAR, CHIPS * own, piece), BF),
            pltpu.VMEM((ZS - 1, NEAR, CHIPS * own, piece), BF),
            pltpu.VMEM((CHIPS * own, piece), BF),
            pltpu.VMEM((CHIPS * own, piece), BF),
            pltpu.VMEM((CHIPS, own, piece), BF),
            pltpu.VMEM((CHIPS - 1, own, piece), BF),
            dma((blocks,)),
            dma((3,)),
            dma((CHIPS + ZS - 1,)),
            dma((CHIPS + ZS - 1,)),
            dma((imgs,)),
            dma((imgs,)),
            dma((imgs,)),
            dma((imgs,)),
            dma((2, imgs)),
            dma((ZS + CHIPS,)),
            dma((ZS + CHIPS,)),
        ],
        compiler_params=pltpu.CompilerParams(
            collective_id=0, has_side_effects=True, vmem_limit_bytes=52 * 2**20
        ),
        name="exchange",
    )(tok, go, so, sp)
    gso_out, gt_out, gp_out = pl.pallas_call(
        settle,
        out_shape=(
            jax.ShapeDtypeStruct((own, blocks, lanes, width), BF),
            jax.ShapeDtypeStruct((imgs, toks, width), BF),
            jax.ShapeDtypeStruct((own, piece), F32),
        ),
        in_specs=[vmem] * 3,
        out_specs=(anywhere,) * 3,
        scratch_shapes=[
            pltpu.VMEM((own * lanes, own * lanes), BF),
            pltpu.VMEM((blocks, own, lanes, width), BF),
            dma((2 + blocks,)),
        ],
        compiler_params=pltpu.CompilerParams(vmem_limit_bytes=20 * 2**20),
        name="settle",
    )(gso, gt, gp)
    return (
        jnp.swapaxes(gt_out, 0, 1),
        gso_out.reshape(own, all_imgs, width),
        gp_out,
    )


def solution(mesh):
    return jax.shard_map(
        per_device,
        mesh=mesh,
        in_specs=(
            P(None, ("dp", "expert"), None),
            P(None, ("dp", "expert"), None),
            P("expert", "dp", None),
            P("expert", None),
        ),
        out_specs=(P(None, ("dp", "expert"), None), P("expert", "dp", None), P("expert", "dp")),
        check_vma=False,
    )
```

time: 264 us -> 160 us (0.61)
  Pallas kernels: 0 us -> 159 us
  waiting for transfers between devices: 159 us -> 0 us
  local copies, waits for them, and re-layouts: 33.9 us -> 0 us
  matrix products: 25.5 us -> 0 us
  starting transfers between devices: 25 us -> 0 us
  between operations: 14.1 us -> 0.64 us
  other arithmetic: 3.8 us -> 0 us
    pallas_call x0 -> x2, Pallas kernels: none -> 159 us  [the longest x1 154 us: per_device(): pl.pallas_call(exchange, out_shape=(pltpu.VMEM((all_imgs, own, width), BF...]
    reduce_scatter x1 -> x0, waiting for transfers between devices: 91.8 us -> none  [per_device(): lax.psum_scatter(param_part.astype(jnp.bfloat16), 'expert', scatter_dimen...]
    all_to_all x4 -> x0, waiting for transfers between devices: 67.4 us -> none  [the longest x1 59 us: fetch_outputs(): lax.all_to_all(shaped, 'expert', split_axis=1, concat_axis=0, tiled=True)]
    dot_general x5 -> x0, matrix products: 25.5 us -> none  [the longest x1 11.5 us: per_device(): jnp.einsum('tbs,tbd->sbd', combine_low, grad_out, preferred_element_type=...]
    all_to_all x4 -> x0, starting transfers between devices: 24.8 us -> none  [the longest x1 8.44 us: sent_to_all(): lax.all_to_all(jnp.broadcast_to(value[None], (length, *value.shape)), axi...]
    unnamed x12 -> x0, local copies, waits for them, and re-layouts: 19.9 us -> none
    reshape x1 -> x0, local copies, waits for them, and re-layouts: 6.72 us -> none  [return_grads(): shaped = grad_slot.reshape(owners, all_slots // owners, img_rows, width)]
    all_to_all x1 -> x0, local copies, waits for them, and re-layouts: 3.65 us -> none  [fetch_outputs(): lax.all_to_all(shaped, 'expert', split_axis=1, concat_axis=0, tiled=True)]
  transfers between devices with their start and end apart: 5 -> 0, of which waited for: 3 -> 0; matrix products, arithmetic and copies ran while one was open for 22% -> 0% of each run, Pallas kernels for 0% -> 0%
where the time goes in v1:
time: 160 us; the launch traced here: 159 us
  Pallas kernels  159 us (99%)
    pallas_call x1, Pallas kernels, per_device(): pl.pallas_call(exchange, out_shape=(pltpu.VMEM((all_imgs, own, width), BF...  154 us
    pallas_call x1, Pallas kernels, per_device(): pl.pallas_call(settle, out_shape=(jax.ShapeDtypeStruct((own, blocks, lane...  4.64 us

profile of v1, /device:TPU:1, one launch (start us, length us, event | category | flops | bytes accessed | tf_op | source)
XLA Modules:
  0.0 159.3 jit_solution(12002728202857436249)
XLA Ops:
  0.6 154.1 %exchange.1 = (bf16[96,32,1024]{2,1,0:T(8,128)(2,1)S(1)}, bf16[6,256,1024]{2,1,0:T(8,128)(2,1)S(1)}, f32[32,128]{1,0:T(8,128)S(1)}) custom-call(bf16[6,256,1024]{2,1,0:T(8,128)(2,1)} %bitcast.7, bf16[6,256,1024]{2,1,0:T(8,128)(2,1)} %bitcast.8, bf16[32,12,8,1024]{3,2,1,0:T(8,128)(2,1)} %bitcast.6, bf16[4,8,1024]{2,1,0:T(8,128)(2,1)} %bitcast.9), custom_call_target="tpu_custom_call" | custom-call | tf_op jit(solution)/shard_map/exchange/pallas_call | solution.py:297
  154.7 4.6 %settle.1 = (bf16[32,12,8,1024]{3,2,1,0:T(8,128)(2,1)}, bf16[6,256,1024]{2,1,0:T(8,128)(2,1)}, f32[32,128]{1,0:T(8,128)}) custom-call(bf16[96,32,1024]{2,1,0:T(8,128)(2,1)S(1)} %get-tuple-element.9.gso, bf16[6,256,1024]{2,1,0:T(8,128)(2,1)S(1)} %get-tuple-element.10.gt, f32[32,128]{1,0:T(8,128)S(1)} %get-tuple-element.11.gp), custom_call_target="tpu_custom_call" | custom-call | tf_op jit(solution)/shard_map/settle/pallas_call | solution.py:343

commit v2 on v1

--- a/solution.py
+++ b/solution.py
@@ -18,6 +18,24 @@
 ORDER = tuple((r, x, c) for c in range(CORES) for r, x in STEPS) + ((0, 0, 1),)
 NT = (((1,), (1,)), ((), ()))
 TN = (((0,), (0,)), ((), ()))
+NN = (((1,), (0,)), ((), ()))
+KINDS = (0, 1, 2)
+HELPER = ((1, 0), (0, 1), (0, 3))
+PARTS = (
+    (((0, 0), (0, 1), (0, 2), (0, 3)), ((0, 0), (1, 0), (0, 3), (1, 3)), ((0, 0), (1, 0), (0, 1), (1, 1))),
+    (((0, 0), (0, 1), (0, 2), (0, 3)), ((0, 0), (1, 0), (0, 1), (1, 1)), ((0, 0), (1, 0), (0, 3), (1, 3))),
+)
+PIECES = 4
+MIX = tuple(kind * 8 + k * CORES + dc for dc in range(CORES) for k in (3, 1, 2, 0) for kind in (0, 1))
+BACK = tuple(tuple(tuple((k, of[k]) for k in (3, 1, 2, 0)) for of in kind) for kind in PARTS)
+
+
+def back(at):
+    return ((ROWS - at[0]) % ROWS, (XS - at[1]) % XS)
+
+
+def add(a, b):
+    return ((a[0] + b[0]) % ROWS, (a[1] + b[1]) % XS)
 
 
 def dot(a, b, dims):
@@ -38,22 +56,27 @@
 def exchange(
     tok_hbm, go_hbm, so_hbm, sp_hbm,
     gso, gt, gp,
-    tok, go, raw, send_a, recv_a, send_b, par, comb, pp, perm,
+    tok, go, raw, send_a, slot_in, send_b, par, comb, low_w, low_s, gc_s, gc_r, gc_all, pp, perm,
     r1s, r1r, acc, r2s, r2r, r3s, r3r, r4s, r4r,
-    so_sem, in_sem, par_s, par_r, as_sem, ar_sem, bs_sem, br_sem, own_sem, red_s, red_r,
+    so_sem, in_sem, par_s, par_r, go_s, go_r, as_sem, ar_sem, bs_sem, br_sem,
+    low_ss, low_rs, gc_ss, gc_rs, own_sem, red_s, red_r,
 ):
-    imgs, width = tok.shape[0], tok.shape[2]
+    imgs, width, tokens = tok.shape[0], tok.shape[2], tok.shape[1]
     blocks, own, lanes = raw.shape[0], so_hbm.shape[0], so_hbm.shape[2]
     slots = CHIPS * CORES * own
-    tokens = tok.shape[1]
+    half = slots // 2
+    rounds = imgs // len(KINDS)
     d = lax.axis_index("dp")
     e = lax.axis_index("expert")
     row, x, c = e // (XS * CORES), (e // CORES) % XS, e % CORES
     chip = e // CORES
     near, z = d // ZS, d % ZS
 
+    def chip_at(dr, dx):
+        return ((row + dr) % ROWS) * XS + (x + dx) % XS
+
     def peer(dr, dx, dc):
-        return ((row + dr) % ROWS) * (XS * CORES) + ((x + dx) % XS) * CORES + (c + dc) % CORES
+        return chip_at(dr, dx) * CORES + (c + dc) % CORES
 
     def zpeer(k):
         return (near * ZS + (z + k) % ZS, e)
@@ -70,13 +93,13 @@
         return pltpu.make_async_copy(so_hbm.at[:, g], raw.at[g], so_sem.at[g])
 
     sp_in = pltpu.make_async_copy(sp_hbm.at[z], par.at[chip, c, z], in_sem.at[0])
-    tok_in = pltpu.make_async_copy(tok_hbm, tok, in_sem.at[1])
-    go_in = pltpu.make_async_copy(go_hbm, go, in_sem.at[2])
+    go_in = pltpu.make_async_copy(go_hbm, go.at[pl.ds(0, imgs)], in_sem.at[1])
+    tok_in = pltpu.make_async_copy(tok_hbm, tok, in_sem.at[2])
     sp_in.start()
+    go_in.start()
     for g in range(blocks):
         load_so(g).start()
     tok_in.start()
-    go_in.start()
     perm[...] = row_order(own, lanes, False)
 
     pl.semaphore_wait(barrier, len(others))
@@ -86,6 +109,9 @@
             src_ref=src, dst_ref=dst, send_sem=s, recv_sem=r, device_id=dev, device_id_type=MESH
         )
 
+    def all_of(ref, sem):
+        return pltpu.make_async_copy(ref, ref, sem)
+
     def par_row(i):
         r, dx = STEPS[i]
         piece = par.at[chip, c, z]
@@ -104,6 +130,21 @@
     sp_in.wait()
     for i in range(len(STEPS)):
         par_row(i).start()
+
+    def helper(t):
+        return (d, peer(*HELPER[t], 0))
+
+    def home(t):
+        return (d, peer(*back(HELPER[t]), 0))
+
+    go_in.wait()
+    step = tokens // PIECES
+    for q in range(PIECES):
+        for j in range(imgs):
+            rows = pl.ds(q * step, step)
+            remote(
+                go.at[j, rows], go.at[imgs + j, rows], go_s.at[j], go_r.at[j], helper(j % len(KINDS))
+            ).start()
 
     @pl.loop(0, blocks)
     def _(g):
@@ -111,31 +152,45 @@
         block = raw.at[g].reshape(own * lanes, width)
         out = send_a.at[pl.ds(g * lanes, lanes)].reshape(own * lanes, width)
         for n in range(0, width, 256):
-            out[:, n : n + 256] = dot(perm[...], block[:, n : n + 256], (((1,), (0,)), ((), ()))).astype(BF)
-
-    def send_out(j, o):
-        p = peer(*o)
-        return remote(
-            send_a.at[p * imgs + j], recv_a.at[j, e], as_sem.at[j], ar_sem.at[j], (d, p)
-        )
-
-    def keep_out(j):
-        return pltpu.make_async_copy(send_a.at[e * imgs + j], recv_a.at[j, e], own_sem.at[0, j])
-
-    def send_back(j, o):
-        p = peer(*o)
-        return remote(
-            send_b.at[j, p], gso.at[e * imgs + j], bs_sem.at[j], br_sem.at[j], (d, p)
-        )
-
-    def keep_back(j):
-        return pltpu.make_async_copy(send_b.at[j, e], gso.at[e * imgs + j], own_sem.at[1, j])
-
-    @pl.loop(0, imgs)
-    def _(j):
-        for o in ORDER:
-            send_out(j, o).start()
-        keep_out(j).start()
+            out[:, n : n + 256] = dot(perm[...], block[:, n : n + 256], NN).astype(BF)
+
+    def out_moves(j, t):
+        for kind in range(2):
+            for k, (dr, dx) in enumerate(PARTS[kind][t]):
+                for dc in range(CORES):
+                    at = back((dr, dx))
+                    hr, hx = at if kind == 0 else add(at, back(HELPER[t]))
+                    image = peer(hr, hx, dc) * imgs + j
+                    yield kind, k, (*at, dc), send_a.at[image], slot_in.at[kind * imgs + j, k, c]
+
+    def send_out(j, t):
+        moves = list(out_moves(j, t))
+        for i in MIX:
+            kind, _, o, src, dst = moves[i]
+            w = kind * imgs + j
+            if o == (0, 0, 0):
+                pltpu.make_async_copy(src, dst, own_sem.at[w]).start()
+            else:
+                remote(src, dst, as_sem.at[j], ar_sem.at[w], (d, peer(*o))).start()
+
+    def wait_out(w):
+        all_of(slot_in.at[w].reshape(2 * len(PARTS[0][0]), own, width).at[pl.ds(0, 7)], ar_sem.at[w]).wait()
+        all_of(send_a.at[0], own_sem.at[w]).wait()
+
+    def send_back(kind, j, t):
+        hr, hx = (0, 0) if kind == 0 else back(HELPER[t])
+        image = peer(hr, hx, 0) * imgs + j
+        w = kind * imgs + j
+        for k, (dr, dx) in BACK[kind][t]:
+            for dc in range(CORES):
+                src, dst = send_b.at[w, k, (c + dc) % CORES], gso.at[image]
+                if (dr, dx, dc) == (0, 0, 0):
+                    pltpu.make_async_copy(src, dst, own_sem.at[2 * imgs + w]).start()
+                else:
+                    remote(src, dst, bs_sem.at[w], br_sem.at[w], (d, peer(dr, dx, dc))).start()
+
+    for t in range(len(KINDS)):
+        send_out(t, t)
 
     for i in range(len(STEPS)):
         par_row(i).wait_recv()
@@ -146,60 +201,108 @@
     par_core().start()
     par_core().wait_recv()
     tok_in.wait()
-    go_in.wait()
 
     params = par.reshape(slots, width)
+
+    def part_chips(kind, t):
+        at = (0, 0) if kind == 0 else HELPER[t]
+        return [chip_at(*add(at, p)) for p in PARTS[kind][t]]
+
+    def send_low(j, t):
+        return remote(low_s.at[j], low_w.at[imgs + j], low_ss.at[j], low_rs.at[j], helper(t))
+
+    @pl.loop(0, rounds)
+    def _(r):
+        for t in range(len(KINDS)):
+            j = r * len(KINDS) + t
+            logits = dot(params[...], tok[j], NT)
+            top = jnp.max(logits, axis=0, keepdims=True)
+            raised = jnp.exp(logits - top)
+            weight = raised / jnp.sum(raised, axis=0, keepdims=True)
+            comb[j] = weight.reshape(CHIPS, CORES * own, tokens)
+            for k, p in enumerate(part_chips(0, t)):
+                low_w[j, k] = comb[j, p].astype(BF)
+            for k, p in enumerate(part_chips(1, t)):
+                low_s[j, k] = comb[j, p].astype(BF)
+            if t > 0:
+                send_low(j - 1, t - 1).start()
+        send_low(r * len(KINDS) + len(KINDS) - 1, len(KINDS) - 1).start()
+
+    for t in range(len(KINDS)):
+        send_out(len(KINDS) + t, t)
+
+    def slot_grads(w):
+        low = low_w[w].reshape(half, tokens)
+        out = send_b.at[w].reshape(half, width)
+        for n in range(0, width, 256):
+            out[:, n : n + 256] = dot(low, go[w, :, n : n + 256], NN).astype(BF)
 
     @pl.loop(0, imgs)
     def _(j):
-        logits = dot(params[...], tok[j], NT)
-        top = jnp.max(logits, axis=0, keepdims=True)
-        raised = jnp.exp(logits - top)
-        weight = raised / jnp.sum(raised, axis=0, keepdims=True)
-        comb[j] = weight
-        low = weight.astype(BF)
-        out = send_b.at[j].reshape(slots, width)
-        for n in range(0, width, 256):
-            out[:, n : n + 256] = dot(low, go[j, :, n : n + 256], (((1,), (0,)), ((), ()))).astype(BF)
-
-        @pl.when(j > 0)
-        def _():
-            for o in ORDER:
-                send_back(j - 1, o).start()
-            keep_back(j - 1).start()
-
-    pp[...] = jnp.zeros_like(pp)
-    for o in ORDER:
-        send_back(imgs - 1, o).start()
-    keep_back(imgs - 1).start()
-
-    def all_of(ref, sem):
-        return pltpu.make_async_copy(ref, ref, sem)
+        slot_grads(j)
+
+    for t in range(len(KINDS)):
+        send_back(0, t, t)
 
     @pl.loop(0, imgs)
     def _(j):
-        all_of(recv_a.at[j, pl.ds(0, len(ORDER))], ar_sem.at[j]).wait()
-        keep_out(j).wait()
-        rows = recv_a.at[j].reshape(slots, width)
-        grad = dot(rows[...], go[j], NT)
-        weight = comb[j]
-        rowdot = jnp.sum(weight * grad, axis=0, keepdims=True)
-        low = (weight * (grad - rowdot)).astype(BF)
-        for n in range(0, width, 256):
-            pp[:, n : n + 256] += dot(low, tok[j, :, n : n + 256], (((1,), (0,)), ((), ())))
-            gt[j, :, n : n + 256] = dot(low, params[:, n : n + 256], TN).astype(BF)
+        all_of(low_w.at[imgs + j], low_rs.at[j]).wait()
+        all_of(go.at[imgs + j], go_r.at[j]).wait()
+        slot_grads(imgs + j)
+
+    def logit_dot(w):
+        return dot(slot_in[w].reshape(half, width), go[w], NT).reshape(-1, CORES * own, tokens)
+
+    def send_gc(j, t):
+        return remote(gc_s.at[j], gc_r.at[j], gc_ss.at[j], gc_rs.at[j], home(t))
+
+    @pl.loop(0, rounds)
+    def _(r):
+        for t in range(len(KINDS)):
+            j = r * len(KINDS) + t
+            wait_out(imgs + j)
+            gc_s[j] = logit_dot(imgs + j).astype(BF)
+            if t > 0:
+                send_gc(j - 1, t - 1).start()
+        send_gc(r * len(KINDS) + len(KINDS) - 1, len(KINDS) - 1).start()
+
+    pp[...] = jnp.zeros_like(pp)
+    for t in range(len(KINDS)):
+        send_back(0, len(KINDS) + t, t)
+    for t in range(len(KINDS)):
+        send_back(1, t, t)
+
+    @pl.loop(0, rounds)
+    def _(r):
+        for t in range(len(KINDS)):
+            j = r * len(KINDS) + t
+            wait_out(j)
+            part = logit_dot(j)
+            for k, p in enumerate(part_chips(0, t)):
+                gc_all[p] = part[k]
+            send_gc(j, t).wait_recv()
+            for k, p in enumerate(part_chips(1, t)):
+                gc_all[p] = gc_r[j, k].astype(F32)
+            grad = gc_all[...].reshape(slots, tokens)
+            weight = comb[j].reshape(slots, tokens)
+            rowdot = jnp.sum(weight * grad, axis=0, keepdims=True)
+            low = (weight * (grad - rowdot)).astype(BF)
+            for n in range(0, width, 256):
+                pp[:, n : n + 256] += dot(low, tok[j, :, n : n + 256], NN)
+                gt[j, :, n : n + 256] = dot(low, params[:, n : n + 256], TN).astype(BF)
 
     share = pp.reshape(CHIPS, CORES, own, width)
     r1s[...] = share[:, 1 - c].astype(BF)
     over_core = remote(r1s, r1r, red_s.at[0], red_r.at[0], partner)
     over_core.start()
+    send_back(1, len(KINDS), 0)
     over_core.wait_recv()
-    half = (share[:, c] + r1r[...].astype(F32)).reshape(CHIPS * own, width)
+    both = (share[:, c] + r1r[...].astype(F32)).reshape(CHIPS * own, width)
     piece = width // (NEAR * ZS)
     for n in range(NEAR):
         for k in range(ZS):
             m = (n * ZS + k) * piece
-            acc[k, n] = half[:, m : m + piece]
+            acc[k, n] = both[:, m : m + piece]
     r2s[...] = acc[...].astype(BF)
 
     def over_z(k):
@@ -215,6 +318,7 @@
     r3s[...] = acc[0, 1 - near].astype(BF)
     over_side = remote(r3s, r3r, red_s.at[ZS], red_r.at[ZS], side)
     over_side.start()
+    send_back(1, len(KINDS) + 1, 1)
     over_side.wait_recv()
     mine = (acc[0, near] + r3r[...].astype(F32)).reshape(CHIPS, own, piece)
     r4s[...] = mine.astype(BF)
@@ -226,6 +330,7 @@
 
     for i in range(len(STEPS)):
         over_chips(i).start()
+    send_back(1, len(KINDS) + 2, 2)
     owned = acc.at[1, 0].reshape(CHIPS, own, piece)[chip]
     for i in range(len(STEPS)):
         over_chips(i).wait_recv()
@@ -244,10 +349,16 @@
 
     @pl.loop(0, imgs)
     def _(j):
-        all_of(send_a.at[pl.ds(0, len(ORDER))], as_sem.at[j]).wait()
-        all_of(send_b.at[j, pl.ds(0, len(ORDER))], bs_sem.at[j]).wait()
-        keep_back(j).wait()
-        all_of(gso.at[pl.ds(0, len(ORDER))], br_sem.at[j]).wait()
+        all_of(go.at[j], go_s.at[j]).wait()
+        all_of(low_s.at[j], low_ss.at[j]).wait()
+        all_of(gc_s.at[j], gc_ss.at[j]).wait()
+        all_of(send_a.at[pl.ds(0, 14)], as_sem.at[j]).wait()
+
+    @pl.loop(0, 2 * imgs)
+    def _(w):
+        all_of(send_a.at[pl.ds(0, 7)], bs_sem.at[w]).wait()
+        all_of(send_a.at[0], own_sem.at[2 * imgs + w]).wait()
+        all_of(gso.at[pl.ds(0, 7)], br_sem.at[w]).wait()
 
 
 def settle(gso, gt, gp, gso_out, gt_out, gp_out, perm, stage, sems):
@@ -293,7 +404,6 @@
     anywhere = pl.BlockSpec(memory_space=pl.ANY)
     vmem = pl.BlockSpec(memory_space=pltpu.VMEM)
     dma = pltpu.SemaphoreType.DMA
-    peers = len(ORDER)
     gso, gt, gp = pl.pallas_call(
         exchange,
         out_shape=(
@@ -305,13 +415,18 @@
         out_specs=(vmem, vmem, vmem),
         scratch_shapes=[
             pltpu.VMEM((imgs, toks, width), BF),
-            pltpu.VMEM((imgs, toks, width), BF),
+            pltpu.VMEM((2 * imgs, toks, width), BF),
             pltpu.VMEM((blocks, own, lanes, width), BF),
             pltpu.VMEM((all_imgs, own, width), BF),
-            pltpu.VMEM((imgs, CHIPS * CORES, own, width), BF),
-            pltpu.VMEM((imgs, CHIPS * CORES, own, width), BF),
+            pltpu.VMEM((2 * imgs, 4, CORES, own, width), BF),
+            pltpu.VMEM((2 * imgs, 4, CORES, own, width), BF),
             pltpu.VMEM((CHIPS, CORES, ZS, own // ZS, width), BF),
-            pltpu.VMEM((imgs, slots, toks), F32),
+            pltpu.VMEM((imgs, CHIPS, CORES * own, toks), F32),
+            pltpu.VMEM((2 * imgs, 4, CORES * own, toks), BF),
+            pltpu.VMEM((imgs, 4, CORES * own, toks), BF),
+            pltpu.VMEM((imgs, 4, CORES * own, toks), BF),
+            pltpu.VMEM((imgs, 4, CORES * own, toks), BF),
+            pltpu.VMEM((CHIPS, CORES * own, toks), F32),
             pltpu.VMEM((slots, width), F32),
             pltpu.VMEM((own * lanes, own * lanes), BF),
             pltpu.VMEM((CHIPS, own, width), BF),
@@ -330,8 +445,14 @@
             dma((imgs,)),
             dma((imgs,)),
             dma((imgs,)),
-            dma((imgs,)),
-            dma((2, imgs)),
+            dma((2 * imgs,)),
+            dma((2 * imgs,)),
+            dma((2 * imgs,)),
+            dma((imgs,)),
+            dma((imgs,)),
+            dma((imgs,)),
+            dma((imgs,)),
+            dma((4 * imgs,)),
             dma((ZS + CHIPS,)),
             dma((ZS + CHIPS,)),
         ],

time: 160 us -> 144 us (0.900)
  Pallas kernels: 159 us -> 143 us
    pallas_call x1, Pallas kernels: 154 us -> 138 us  [per_device(): pl.pallas_call(exchange, out_shape=(pltpu.VMEM((all_imgs, own, width), BF...]
where the time goes in v2:
time: 144 us
  Pallas kernels  143 us (99%)
    pallas_call x1, Pallas kernels, per_device(): pl.pallas_call(exchange, out_shape=(pltpu.VMEM((all_imgs, own, width), BF...  138 us
    pallas_call x1, Pallas kernels, per_device(): pl.pallas_call(settle, out_shape=(jax.ShapeDtypeStruct((own, blocks, lane...  4.64 us

profile of v2, /device:TPU:1, one launch (start us, length us, event | category | flops | bytes accessed | tf_op | source)
XLA Modules:
  0.0 143.6 jit_solution(6633284983649416684)
XLA Ops:
  0.6 138.4 %exchange.1 = (bf16[96,32,1024]{2,1,0:T(8,128)(2,1)S(1)}, bf16[6,256,1024]{2,1,0:T(8,128)(2,1)S(1)}, f32[32,128]{1,0:T(8,128)S(1)}) custom-call(bf16[6,256,1024]{2,1,0:T(8,128)(2,1)} %bitcast.7, bf16[6,256,1024]{2,1,0:T(8,128)(2,1)} %bitcast.8, bf16[32,12,8,1024]{3,2,1,0:T(8,128)(2,1)} %bitcast.6, bf16[4,8,1024]{2,1,0:T(8,128)(2,1)} %bitcast.9), custom_call_target="tpu_custom_call" | custom-call | tf_op jit(solution)/shard_map/exchange/pallas_call | solution.py:407
  139.0 4.6 %settle.1 = (bf16[32,12,8,1024]{3,2,1,0:T(8,128)(2,1)}, bf16[6,256,1024]{2,1,0:T(8,128)(2,1)}, f32[32,128]{1,0:T(8,128)}) custom-call(bf16[96,32,1024]{2,1,0:T(8,128)(2,1)S(1)} %get-tuple-element.9.gso, bf16[6,256,1024]{2,1,0:T(8,128)(2,1)S(1)} %get-tuple-element.10.gt, f32[32,128]{1,0:T(8,128)S(1)} %get-tuple-element.11.gp), custom_call_target="tpu_custom_call" | custom-call | tf_op jit(solution)/shard_map/settle/pallas_call | solution.py:464

commit v3 on v2

--- a/solution.py
+++ b/solution.py
@@ -163,10 +163,12 @@
                     image = peer(hr, hx, dc) * imgs + j
                     yield kind, k, (*at, dc), send_a.at[image], slot_in.at[kind * imgs + j, k, c]
 
-    def send_out(j, t):
+    def send_out(j, t, kinds):
         moves = list(out_moves(j, t))
         for i in MIX:
             kind, _, o, src, dst = moves[i]
+            if kind not in kinds:
+                continue
             w = kind * imgs + j
             if o == (0, 0, 0):
                 pltpu.make_async_copy(src, dst, own_sem.at[w]).start()
@@ -181,8 +183,8 @@
         hr, hx = (0, 0) if kind == 0 else back(HELPER[t])
         image = peer(hr, hx, 0) * imgs + j
         w = kind * imgs + j
-        for k, (dr, dx) in BACK[kind][t]:
-            for dc in range(CORES):
+        for dc in range(CORES):
+            for k, (dr, dx) in BACK[kind][t]:
                 src, dst = send_b.at[w, k, (c + dc) % CORES], gso.at[image]
                 if (dr, dx, dc) == (0, 0, 0):
                     pltpu.make_async_copy(src, dst, own_sem.at[2 * imgs + w]).start()
@@ -190,7 +192,7 @@
                     remote(src, dst, bs_sem.at[w], br_sem.at[w], (d, peer(dr, dx, dc))).start()
 
     for t in range(len(KINDS)):
-        send_out(t, t)
+        send_out(t, t, (0, 1))
 
     for i in range(len(STEPS)):
         par_row(i).wait_recv()
@@ -228,8 +230,9 @@
                 send_low(j - 1, t - 1).start()
         send_low(r * len(KINDS) + len(KINDS) - 1, len(KINDS) - 1).start()
 
-    for t in range(len(KINDS)):
-        send_out(len(KINDS) + t, t)
+    for kind in (1, 0):
+        for t in range(len(KINDS)):
+            send_out(len(KINDS) + t, t, (kind,))
 
     def slot_grads(w):
         low = low_w[w].reshape(half, tokens)
@@ -241,15 +244,6 @@
     def _(j):
         slot_grads(j)
 
-    for t in range(len(KINDS)):
-        send_back(0, t, t)
-
-    @pl.loop(0, imgs)
-    def _(j):
-        all_of(low_w.at[imgs + j], low_rs.at[j]).wait()
-        all_of(go.at[imgs + j], go_r.at[j]).wait()
-        slot_grads(imgs + j)
-
     def logit_dot(w):
         return dot(slot_in[w].reshape(half, width), go[w], NT).reshape(-1, CORES * own, tokens)
 
@@ -260,17 +254,18 @@
     def _(r):
         for t in range(len(KINDS)):
             j = r * len(KINDS) + t
+            all_of(low_w.at[imgs + j], low_rs.at[j]).wait()
+            all_of(go.at[imgs + j], go_r.at[j]).wait()
+            slot_grads(imgs + j)
             wait_out(imgs + j)
             gc_s[j] = logit_dot(imgs + j).astype(BF)
             if t > 0:
                 send_gc(j - 1, t - 1).start()
         send_gc(r * len(KINDS) + len(KINDS) - 1, len(KINDS) - 1).start()
 
+    for j in range(imgs):
+        send_back(0, j, j % len(KINDS))
     pp[...] = jnp.zeros_like(pp)
-    for t in range(len(KINDS)):
-        send_back(0, len(KINDS) + t, t)
-    for t in range(len(KINDS)):
-        send_back(1, t, t)
 
     @pl.loop(0, rounds)
     def _(r):
@@ -294,8 +289,9 @@
     share = pp.reshape(CHIPS, CORES, own, width)
     r1s[...] = share[:, 1 - c].astype(BF)
     over_core = remote(r1s, r1r, red_s.at[0], red_r.at[0], partner)
+    for t in (0, 1):
+        send_back(1, t, t)
     over_core.start()
-    send_back(1, len(KINDS), 0)
     over_core.wait_recv()
     both = (share[:, c] + r1r[...].astype(F32)).reshape(CHIPS * own, width)
     piece = width // (NEAR * ZS)
@@ -318,7 +314,8 @@
     r3s[...] = acc[0, 1 - near].astype(BF)
     over_side = remote(r3s, r3r, red_s.at[ZS], red_r.at[ZS], side)
     over_side.start()
-    send_back(1, len(KINDS) + 1, 1)
+    send_back(1, 2, 2)
+    send_back(1, len(KINDS), 0)
     over_side.wait_recv()
     mine = (acc[0, near] + r3r[...].astype(F32)).reshape(CHIPS, own, piece)
     r4s[...] = mine.astype(BF)
@@ -330,7 +327,8 @@
 
     for i in range(len(STEPS)):
         over_chips(i).start()
-    send_back(1, len(KINDS) + 2, 2)
+    for t in (1, 2):
+        send_back(1, len(KINDS) + t, t)
     owned = acc.at[1, 0].reshape(CHIPS, own, piece)[chip]
     for i in range(len(STEPS)):
         over_chips(i).wait_recv()
@@ -374,13 +372,14 @@
     def put(g):
         return pltpu.make_async_copy(stage.at[g], gso_out.at[:, g], sems.at[2 + g])
 
-    @pl.loop(0, blocks)
-    def _(g):
-        block = gso.at[pl.ds(g * lanes, lanes)].reshape(own * lanes, width)
-        out = stage.at[g].reshape(own * lanes, width)
-        for n in range(0, width, 256):
-            out[:, n : n + 256] = dot(perm[...], block[:, n : n + 256], (((1,), (0,)), ((), ()))).astype(BF)
-        put(g).start()
+    @pl.loop(0, blocks // 4)
+    def _(h):
+        for g in range(4):
+            block = gso.at[pl.ds((h * 4 + g) * lanes, lanes)].reshape(own * lanes, width)
+            out = stage.at[h * 4 + g].reshape(own * lanes, width)
+            out[...] = dot(perm[...], block[...], NN).astype(BF)
+        for g in range(4):
+            put(h * 4 + g).start()
 
     @pl.loop(0, blocks)
     def _(g):

time: 144 us -> 142 us (0.986)
  Pallas kernels: 143 us -> 141 us
where the time goes in v3:
time: 142 us
  Pallas kernels  141 us (99%)
    pallas_call x1, Pallas kernels, per_device(): pl.pallas_call(exchange, out_shape=(pltpu.VMEM((all_imgs, own, width), BF...  137 us
    pallas_call x1, Pallas kernels, per_device(): pl.pallas_call(settle, out_shape=(jax.ShapeDtypeStruct((own, blocks, lane...  3.72 us

profile of v3, /device:TPU:1, one launch (start us, length us, event | category | flops | bytes accessed | tf_op | source)
XLA Modules:
  0.0 141.7 jit_solution(6428909145973048439)
XLA Ops:
  0.6 137.4 %exchange.1 = (bf16[96,32,1024]{2,1,0:T(8,128)(2,1)S(1)}, bf16[6,256,1024]{2,1,0:T(8,128)(2,1)S(1)}, f32[32,128]{1,0:T(8,128)S(1)}) custom-call(bf16[6,256,1024]{2,1,0:T(8,128)(2,1)} %bitcast.7, bf16[6,256,1024]{2,1,0:T(8,128)(2,1)} %bitcast.8, bf16[32,12,8,1024]{3,2,1,0:T(8,128)(2,1)} %bitcast.6, bf16[4,8,1024]{2,1,0:T(8,128)(2,1)} %bitcast.9), custom_call_target="tpu_custom_call" | custom-call | tf_op jit(solution)/shard_map/exchange/pallas_call | solution.py:406
  138.0 3.7 %settle.1 = (bf16[32,12,8,1024]{3,2,1,0:T(8,128)(2,1)}, bf16[6,256,1024]{2,1,0:T(8,128)(2,1)}, f32[32,128]{1,0:T(8,128)}) custom-call(bf16[96,32,1024]{2,1,0:T(8,128)(2,1)S(1)} %get-tuple-element.9.gso, bf16[6,256,1024]{2,1,0:T(8,128)(2,1)S(1)} %get-tuple-element.10.gt, f32[32,128]{1,0:T(8,128)S(1)} %get-tuple-element.11.gp), custom_call_target="tpu_custom_call" | custom-call | tf_op jit(solution)/shard_map/settle/pallas_call | solution.py:463

commit v4 on v3

--- a/solution.py
+++ b/solution.py
@@ -179,17 +179,19 @@
         all_of(slot_in.at[w].reshape(2 * len(PARTS[0][0]), own, width).at[pl.ds(0, 7)], ar_sem.at[w]).wait()
         all_of(send_a.at[0], own_sem.at[w]).wait()
 
-    def send_back(kind, j, t):
-        hr, hx = (0, 0) if kind == 0 else back(HELPER[t])
-        image = peer(hr, hx, 0) * imgs + j
-        w = kind * imgs + j
-        for dc in range(CORES):
-            for k, (dr, dx) in BACK[kind][t]:
-                src, dst = send_b.at[w, k, (c + dc) % CORES], gso.at[image]
-                if (dr, dx, dc) == (0, 0, 0):
-                    pltpu.make_async_copy(src, dst, own_sem.at[2 * imgs + w]).start()
-                else:
-                    remote(src, dst, bs_sem.at[w], br_sem.at[w], (d, peer(dr, dx, dc))).start()
+    def send_back(kind, r, dcs):
+        for dc in dcs:
+            for i in range(4):
+                for t in range(len(KINDS)):
+                    j = r * len(KINDS) + t
+                    hr, hx = (0, 0) if kind == 0 else back(HELPER[t])
+                    w = kind * imgs + j
+                    k, (dr, dx) = BACK[kind][t][i]
+                    src, dst = send_b.at[w, k, (c + dc) % CORES], gso.at[peer(hr, hx, 0) * imgs + j]
+                    if (dr, dx, dc) == (0, 0, 0):
+                        pltpu.make_async_copy(src, dst, own_sem.at[2 * imgs + w]).start()
+                    else:
+                        remote(src, dst, bs_sem.at[w], br_sem.at[w], (d, peer(dr, dx, dc))).start()
 
     for t in range(len(KINDS)):
         send_out(t, t, (0, 1))
@@ -263,8 +265,8 @@
                 send_gc(j - 1, t - 1).start()
         send_gc(r * len(KINDS) + len(KINDS) - 1, len(KINDS) - 1).start()
 
-    for j in range(imgs):
-        send_back(0, j, j % len(KINDS))
+    for r in range(rounds):
+        send_back(0, r, (0, 1))
     pp[...] = jnp.zeros_like(pp)
 
     @pl.loop(0, rounds)
@@ -289,8 +291,7 @@
     share = pp.reshape(CHIPS, CORES, own, width)
     r1s[...] = share[:, 1 - c].astype(BF)
     over_core = remote(r1s, r1r, red_s.at[0], red_r.at[0], partner)
-    for t in (0, 1):
-        send_back(1, t, t)
+    send_back(1, 0, (0, 1))
     over_core.start()
     over_core.wait_recv()
     both = (share[:, c] + r1r[...].astype(F32)).reshape(CHIPS * own, width)
@@ -314,8 +315,7 @@
     r3s[...] = acc[0, 1 - near].astype(BF)
     over_side = remote(r3s, r3r, red_s.at[ZS], red_r.at[ZS], side)
     over_side.start()
-    send_back(1, 2, 2)
-    send_back(1, len(KINDS), 0)
+    send_back(1, 1, (0,))
     over_side.wait_recv()
     mine = (acc[0, near] + r3r[...].astype(F32)).reshape(CHIPS, own, piece)
     r4s[...] = mine.astype(BF)
@@ -327,8 +327,7 @@
 
     for i in range(len(STEPS)):
         over_chips(i).start()
-    for t in (1, 2):
-        send_back(1, len(KINDS) + t, t)
+    send_back(1, 1, (1,))
     owned = acc.at[1, 0].reshape(CHIPS, own, piece)[chip]
     for i in range(len(STEPS)):
         over_chips(i).wait_recv()

time: 142 us -> 142 us (level)
  no operation moved by 1% of the time
where the time goes in v4:
time: 142 us
  Pallas kernels  141 us (99%)
    pallas_call x1, Pallas kernels, per_device(): pl.pallas_call(exchange, out_shape=(pltpu.VMEM((all_imgs, own, width), BF...  137 us
    pallas_call x1, Pallas kernels, per_device(): pl.pallas_call(settle, out_shape=(jax.ShapeDtypeStruct((own, blocks, lane...  3.72 us

profile of v4, /device:TPU:1, one launch (start us, length us, event | category | flops | bytes accessed | tf_op | source)
XLA Modules:
  0.0 141.6 jit_solution(17166817912272268151)
XLA Ops:
  0.6 137.3 %exchange.1 = (bf16[96,32,1024]{2,1,0:T(8,128)(2,1)S(1)}, bf16[6,256,1024]{2,1,0:T(8,128)(2,1)S(1)}, f32[32,128]{1,0:T(8,128)S(1)}) custom-call(bf16[6,256,1024]{2,1,0:T(8,128)(2,1)} %bitcast.7, bf16[6,256,1024]{2,1,0:T(8,128)(2,1)} %bitcast.8, bf16[32,12,8,1024]{3,2,1,0:T(8,128)(2,1)} %bitcast.6, bf16[4,8,1024]{2,1,0:T(8,128)(2,1)} %bitcast.9), custom_call_target="tpu_custom_call" | custom-call | tf_op jit(solution)/shard_map/exchange/pallas_call | solution.py:405
  137.9 3.7 %settle.1 = (bf16[32,12,8,1024]{3,2,1,0:T(8,128)(2,1)}, bf16[6,256,1024]{2,1,0:T(8,128)(2,1)}, f32[32,128]{1,0:T(8,128)}) custom-call(bf16[96,32,1024]{2,1,0:T(8,128)(2,1)S(1)} %get-tuple-element.9.gso, bf16[6,256,1024]{2,1,0:T(8,128)(2,1)S(1)} %get-tuple-element.10.gt, f32[32,128]{1,0:T(8,128)S(1)} %get-tuple-element.11.gp), custom_call_target="tpu_custom_call" | custom-call | tf_op jit(solution)/shard_map/settle/pallas_call | solution.py:462

commit v5 on v4

--- a/solution.py
+++ b/solution.py
@@ -26,6 +26,7 @@
     (((0, 0), (0, 1), (0, 2), (0, 3)), ((0, 0), (1, 0), (0, 1), (1, 1)), ((0, 0), (1, 0), (0, 3), (1, 3))),
 )
 PIECES = 4
+CLOSE = ((1, 0, 0), (0, 1, 0), (0, 3, 0), (0, 0, 1))
 MIX = tuple(kind * 8 + k * CORES + dc for dc in range(CORES) for k in (3, 1, 2, 0) for kind in (0, 1))
 BACK = tuple(tuple(tuple((k, of[k]) for k in (3, 1, 2, 0)) for of in kind) for kind in PARTS)
 
@@ -59,7 +60,7 @@
     tok, go, raw, send_a, slot_in, send_b, par, comb, low_w, low_s, gc_s, gc_r, gc_all, pp, perm,
     r1s, r1r, acc, r2s, r2r, r3s, r3r, r4s, r4r,
     so_sem, in_sem, par_s, par_r, go_s, go_r, as_sem, ar_sem, bs_sem, br_sem,
-    low_ss, low_rs, gc_ss, gc_rs, own_sem, red_s, red_r,
+    low_ss, low_rs, gc_ss, gc_rs, own_sem, red_s, red_r, ready,
 ):
     imgs, width, tokens = tok.shape[0], tok.shape[2], tok.shape[1]
     blocks, own, lanes = raw.shape[0], so_hbm.shape[0], so_hbm.shape[2]
@@ -85,7 +86,8 @@
     partner = (d, peer(0, 0, 1))
 
     barrier = pltpu.get_barrier_semaphore()
-    others = [(d, peer(*o)) for o in ORDER] + [zpeer(k) for k in range(1, ZS)] + [side]
+    close = [(d, peer(*o)) for o in CLOSE]
+    others = close + [zpeer(k) for k in range(1, ZS)] + [side]
     for dev in others:
         pl.semaphore_signal(barrier, inc=1, device_id=dev, device_id_type=MESH)
 
@@ -127,24 +129,30 @@
         n = len(STEPS) + ZS - 1
         return remote(piece, piece, par_s.at[n], par_r.at[n], partner)
 
+    def helper(t):
+        return (d, peer(*HELPER[t], 0))
+
+    def home(t):
+        return (d, peer(*back(HELPER[t]), 0))
+
+    def send_go(q):
+        rows = pl.ds(q * (tokens // PIECES), tokens // PIECES)
+        for j in range(imgs):
+            remote(
+                go.at[j, rows], go.at[imgs + j, rows], go_s.at[j], go_r.at[j], helper(j % len(KINDS))
+            ).start()
+
+    go_in.wait()
+    send_go(0)
+    for i in range(len(CLOSE) - 1):
+        for dev in close:
+            pl.semaphore_signal(ready.at[i], inc=1, device_id=dev, device_id_type=MESH)
+        pl.semaphore_wait(ready.at[i], len(close))
     sp_in.wait()
     for i in range(len(STEPS)):
         par_row(i).start()
-
-    def helper(t):
-        return (d, peer(*HELPER[t], 0))
-
-    def home(t):
-        return (d, peer(*back(HELPER[t]), 0))
-
-    go_in.wait()
-    step = tokens // PIECES
-    for q in range(PIECES):
-        for j in range(imgs):
-            rows = pl.ds(q * step, step)
-            remote(
-                go.at[j, rows], go.at[imgs + j, rows], go_s.at[j], go_r.at[j], helper(j % len(KINDS))
-            ).start()
+    for q in range(1, PIECES):
+        send_go(q)
 
     @pl.loop(0, blocks)
     def _(g):
@@ -453,6 +461,7 @@
             dma((4 * imgs,)),
             dma((ZS + CHIPS,)),
             dma((ZS + CHIPS,)),
+            pltpu.SemaphoreType.REGULAR((len(CLOSE) - 1,)),
         ],
         compiler_params=pltpu.CompilerParams(
             collective_id=0, has_side_effects=True, vmem_limit_bytes=52 * 2**20

time: 142 us -> 142 us (level)
  no operation moved by 1% of the time
where the time goes in v5:
time: 142 us
  Pallas kernels  141 us (99%)
    pallas_call x1, Pallas kernels, per_device(): pl.pallas_call(exchange, out_shape=(pltpu.VMEM((all_imgs, own, width), BF...  137 us
    pallas_call x1, Pallas kernels, per_device(): pl.pallas_call(settle, out_shape=(jax.ShapeDtypeStruct((own, blocks, lane...  3.72 us

profile of v5, /device:TPU:1, one launch (start us, length us, event | category | flops | bytes accessed | tf_op | source)
XLA Modules:
  0.0 141.6 jit_solution(9167114939001993674)
XLA Ops:
  0.6 137.2 %exchange.1 = (bf16[96,32,1024]{2,1,0:T(8,128)(2,1)S(1)}, bf16[6,256,1024]{2,1,0:T(8,128)(2,1)S(1)}, f32[32,128]{1,0:T(8,128)S(1)}) custom-call(bf16[6,256,1024]{2,1,0:T(8,128)(2,1)} %bitcast.7, bf16[6,256,1024]{2,1,0:T(8,128)(2,1)} %bitcast.8, bf16[32,12,8,1024]{3,2,1,0:T(8,128)(2,1)} %bitcast.6, bf16[4,8,1024]{2,1,0:T(8,128)(2,1)} %bitcast.9), custom_call_target="tpu_custom_call" | custom-call | tf_op jit(solution)/shard_map/exchange/pallas_call | solution.py:413
  137.8 3.7 %settle.1 = (bf16[32,12,8,1024]{3,2,1,0:T(8,128)(2,1)}, bf16[6,256,1024]{2,1,0:T(8,128)(2,1)}, f32[32,128]{1,0:T(8,128)}) custom-call(bf16[96,32,1024]{2,1,0:T(8,128)(2,1)S(1)} %get-tuple-element.9.gso, bf16[6,256,1024]{2,1,0:T(8,128)(2,1)S(1)} %get-tuple-element.10.gt, f32[32,128]{1,0:T(8,128)S(1)} %get-tuple-element.11.gp), custom_call_target="tpu_custom_call" | custom-call | tf_op jit(solution)/shard_map/settle/pallas_call | solution.py:471
